TPU v7x, 768 devices: a whole 4x8x12 slice. The times are simulated.
768 devices in a mesh: dp: 12 (over z), rep: 8 (over y), grp: 8 (over x, core).
Axes of the slice: x: 4, y: 8, z: 12, core: 2. Of those that a mesh axis runs over, the one named last changes fastest.
Arguments:
- grad_parts: float32 [64, 24, 192, 2048], P(('rep', 'grp'), None, 'dp'), may hold values from -16 to 16
- momentum: float32 [24, 192, 2048], P(None, 'dp', ('rep', 'grp')), may hold values from -24 to 24
- layer_live: int32 [24], replicated, may hold values from 0 to 1, as said below
Outputs:
- new_momentum: float32 [24, 192, 2048], P(None, 'dp', ('rep', 'grp'))
- orth_update: bfloat16 [24, 192, 2048], P(None, 'dp', ('rep', 'grp'))
Inputs may be any that keep to these rules, and one draw needn't show every extreme that they name: `layer_live`: at least one matrix is live in every draw.
All inputs are finite; a program needn't handle non-finite values.
Results may differ from a plain program's by a relative error of at most 0.028.
Values may be sent and summed in bfloat16 or wider, within the bound.
No kernel may reach another device: no remote copies, remote signals or barrier semaphores. Data moves between devices by JAX's collectives and lax.ppermute only.
A program may use at most 64 MiB of HBM per device.

v0:
```python
import math

import jax
import jax.numpy as jnp
from jax import lax
from jax.sharding import Mesh
from jax.sharding import PartitionSpec as P

ITERS = 5
REP_GRP = ("rep", "grp_0", "grp_1")


decay_rate = 0.95
first_coef = 3.4445
second_coef = -4.775
third_coef = 2.0315
norm_eps = 1e-07


def sum_by_axis(shard, axes, dim):
    if not axes:
        return shard
    nearer = lax.psum_scatter(shard, axes[0], scatter_dimension=dim, tiled=True)
    return sum_by_axis(nearer, axes[1:], dim)


def laid_out(blocks, dim):
    blocks = jnp.moveaxis(blocks, 0, dim)
    shape = blocks.shape
    return blocks.reshape(*shape[:dim], shape[dim] * shape[dim + 1], *shape[dim + 2 :])


def all_blocks(shard, axes, turns):
    blocks = shard[None]
    for k in turns:
        blocks = lax.all_gather(blocks, axes[k], axis=0, tiled=True)
    current = [lax.axis_size(axes[k]) for k in reversed(turns)]
    blocks = blocks.reshape(*current, *shard.shape)
    turned = sorted(range(len(turns)), key=lambda place: turns[len(turns) - 1 - place])
    return blocks.transpose(*turned, *range(len(turns), blocks.ndim)).reshape(-1, *shard.shape)


def gathered_by_axis(shard, axes, turns, dim):
    return laid_out(all_blocks(shard, axes, turns), dim)


def newton_schulz(source):
    source_f32 = source.astype(jnp.float32)
    frob_norm = jnp.sqrt(jnp.sum(source_f32 * source_f32))
    current = (source_f32 / (frob_norm + norm_eps)).astype(jnp.bfloat16)
    next_iterate = source_f32
    for iteration in range(ITERS):
        gram_matrix = lax.dot_general(
            current, current, (((1,), (1,)), ((), ())), preferred_element_type=jnp.float32
        ).astype(jnp.bfloat16)
        squared = jnp.dot(gram_matrix, gram_matrix, preferred_element_type=jnp.float32)
        polynomial = (second_coef * gram_matrix.astype(jnp.float32) + third_coef * squared).astype(
            jnp.bfloat16
        )
        next_iterate = first_coef * current.astype(jnp.float32) + jnp.dot(
            polynomial, current, preferred_element_type=jnp.float32
        )
        if iteration + 1 < ITERS:
            current = next_iterate.astype(jnp.bfloat16)
    return (next_iterate * math.sqrt(source.shape[1])).astype(jnp.bfloat16)


def zero_result(matrix):
    return jnp.zeros_like(matrix)


def guarded(matrix):
    return lax.cond(jnp.any(matrix != 0), newton_schulz, zero_result, matrix)


def per_device(grad_parts, momentum, layer_live):
    width = momentum.shape[2]
    col_start = lax.axis_index(REP_GRP) * width
    active = (layer_live > 0)[:, None, None]
    summed_share = sum_by_axis(grad_parts[0], REP_GRP, 2)
    fresh_momentum = jnp.where(active, decay_rate * momentum + summed_share, momentum)
    sources = gathered_by_axis(fresh_momentum.astype(jnp.bfloat16), REP_GRP, (1, 0, 2), 2)
    owners = lax.axis_size("dp")
    matrices = layer_live.shape[0]
    per_owner = matrices // owners
    piece_rows = sources.shape[1]
    col_count = sources.shape[2]
    matrix_ids = jnp.arange(matrices, dtype=jnp.int32)
    live_flag = (layer_live > 0).astype(jnp.int32)
    live_rank = jnp.cumsum(live_flag) - 1
    slot_pos = jnp.where(live_flag > 0, live_rank, -1)
    slot_ids = jnp.arange(matrices, dtype=jnp.int32)
    placing = slot_pos[None, :] == slot_ids[:, None]
    holder = jnp.sum(jnp.where(placing, matrix_ids[None, :], 0), axis=1)
    filled = jnp.sum(placing.astype(jnp.int32) * live_flag[None, :], axis=1)
    picked_rows = jnp.take(sources, holder, axis=0)
    outgoing = jnp.where(filled[:, None, None] > 0, picked_rows, jnp.zeros_like(picked_rows))
    outgoing = outgoing.reshape(per_owner, owners, piece_rows, col_count)
    blocks = lax.all_to_all(outgoing, "dp", split_axis=1, concat_axis=1, tiled=True)
    item_count = blocks.shape[0]
    stacked = blocks.reshape(item_count, owners * piece_rows, col_count)
    results = lax.map(guarded, stacked)
    results = results.reshape(item_count, owners, piece_rows, col_count)
    returned = lax.all_to_all(results, "dp", split_axis=1, concat_axis=1, tiled=True)
    returned = returned.reshape(matrices, piece_rows, col_count)
    own_cols = lax.dynamic_slice_in_dim(returned, col_start, width, 2)
    gathered = jnp.take(own_cols, jnp.maximum(slot_pos, 0), axis=0)
    orth_update = jnp.where(active, gathered, jnp.zeros_like(gathered))
    return (fresh_momentum, orth_update)


def solution(mesh):
    torus = Mesh(
        mesh.devices.reshape(mesh.shape["dp"], mesh.shape["rep"], 4, 2),
        ("dp", "rep", "grp_0", "grp_1"),
    )
    placed = (P(REP_GRP, None, "dp", None), P(None, "dp", REP_GRP), P())
    return jax.shard_map(
        per_device,
        mesh=torus,
        in_specs=placed,
        out_specs=(P(None, "dp", REP_GRP), P(None, "dp", REP_GRP)),
        check_vma=False,
    )
```

profile of v0, /device:TPU:2, one launch (start us, length us, event | category | flops | bytes accessed | tf_op | source)
XLA Modules:
  0.0 385.9 jit_solution(3984879105785745902)
XLA Ops:
  7.9 62.0 %reduce-scatter.8.cloned.1.call-done = f32[24,16,256]{2,1,0:T(8,128)} async-done(((f32[24,16,2048]{2,1,0:T(8,128)}), f32[24,16,256]{2,1,0:T(8,128)}) %reduce-scatter.8.cloned.1.call-update) | async-done | bytes 393232 | tf_op jit(solution)/shard_map/reduce_scatter | solution.py:23
  69.9 2.0 copy.36
  72.0 1.6 reshape.112
  73.9 28.7 %reduce-scatter.10.cloned.1.call-done = f32[64,384]{1,0:T(8,128)} async-done(((f32[256,384]{1,0:T(8,128)}), f32[64,384]{1,0:T(8,128)}) %reduce-scatter.10.cloned.1.call-update) | async-done | bytes 98320
  102.7 21.6 %reduce-scatter.12.cloned.1.call-done = f32[32,384]{1,0:T(8,128)} async-done(((f32[64,384]{1,0:T(8,128)}), f32[32,384]{1,0:T(8,128)}) %reduce-scatter.12.cloned.1.call-update) | async-done | bytes 49168
  126.2 12.5 %all-gather = bf16[96,16,32]{2,1,0:T(8,128)(2,1)S(1)} all-gather(bf16[24,16,32]{2,1,0:T(8,128)(2,1)S(1)} %get-tuple-element.37), channel_id=2, replica_groups=mesh['dp'=12,'rep'=8,'grp_0'=4,'grp_1'=2] {'grp_0'}, dimensions={0}, use_global_device_ids=true | all-gather | bytes 122880 | tf_op jit(solution)/shard_map/all_gather | solution.py:36
  138.8 36.9 %all_gather.10 = bf16[32,24,16,32]{3,2,1,0:T(8,128)(2,1)} all-gather(bf16[4,24,16,32]{3,2,1,0:T(8,128)(2,1)S(1)} %bitcast.61), channel_id=1, replica_groups=mesh['dp'=12,'rep'=8,'grp_0'=4,'grp_1'=2] {'rep'}, dimensions={0}, use_global_device_ids=true | all-gather | bytes 884736 | tf_op jit(solution)/shard_map/all_gather | solution.py:36
  176.3 26.5 %all-gather.3.cloned.1.call-done = bf16[64,24,16,32]{3,2,1,0:T(8,128)(2,1)} async-done(((bf16[32,24,16,32]{3,2,1,0:T(8,128)(2,1)}), bf16[64,24,16,32]{3,2,1,0:T(8,128)(2,1)}) %all-gather.3.cloned.1.call-update) | async-done | bytes 1572880 | tf_op jit(solution)/shard_map/all_gather | solution.py:36
  202.7 3.9 %copy.30 = bf16[8,4,2,24,16,32]{5,4,3,2,1,0:T(8,128)(2,1)S(1)} copy(bf16[8,4,2,24,16,32]{5,4,3,1,0,2:T(8,128)(2,1)} %bitcast.55) | data formatting | bytes 3145728 | tf_op jit(solution)/shard_map/transpose | solution.py:40
  206.6 6.7 %copy.31 = bf16[24,16,64,32]{3,2,1,0:T(8,128)(2,1)} copy(bf16[24,16,64,32]{3,1,0,2:T(8,128)(2,1)S(1)} %bitcast.52) | data formatting | bytes 3145728 | tf_op jit(solution)/shard_map/transpose | solution.py:28
  213.3 8.5 %reshape.90 = bf16[24,16,2048]{2,1,0:T(8,128)(2,1)S(1)} reshape(bf16[24,16,64,32]{3,2,1,0:T(8,128)(2,1)} %copy.31) | data formatting | bytes 3145728 | tf_op jit(solution)/shard_map/reshape | solution.py:30
  222.5 1.4 fusion.51
  223.9 10.2 %all-to-all-start = ((bf16[2,12,16,2048]{3,2,0,1:T(8,128)(2,1)}), bf16[2,12,16,2048]{3,2,0,1:T(8,128)(2,1)}, u32[]{:S(2)}, u32[]{:S(2)}) async-start(bf16[2,12,16,2048]{3,2,0,1:T(8,128)(2,1)} %fusion.51), calls=%async_computation.1 | async-start | bytes 3145728 | tf_op jit(solution)/shard_map/all_to_all | solution.py:99
  234.2 58.4 %all-to-all-done = bf16[2,12,16,2048]{3,2,0,1:T(8,128)(2,1)} async-done(((bf16[2,12,16,2048]{3,2,0,1:T(8,128)(2,1)}), bf16[2,12,16,2048]{3,2,0,1:T(8,128)(2,1)}, u32[]{:S(2)}, u32[]{:S(2)}) %all-to-all-start) | async-done | bytes 1572896 | tf_op jit(solution)/shard_map/all_to_all | solution.py:99
  292.5 1.5 copy.33
  294.0 19.4 %while.10 = (s32[]{:T(128)}, bf16[2,192,2048]{2,1,0:T(8,128)(2,1)}, bf16[2,192,2048]{2,1,0:T(8,128)(2,1)S(1)}, s32[]{:T(128)}) while((s32[]{:T(128)}, bf16[2,192,2048]{2,1,0:T(8,128)(2,1)}, bf16[2,192,2048]{2,1,0:T(8,128)(2,1)S(1)}, s32[]{:T(128)}) %tuple.53), condition=%wide.region_11.12_spmd, body=%wide.region_6.11_spmd.sunk | while | flops 1595596800 | bytes 29049504 | solution.py:102
  294.1 1.1 compare_reduce_fusion.2
  295.8 6.3 %conditional.2 = (bf16[1,192,2048]{2,1,0:T(8,128)(2,1)S(1)}) conditional(s32[]{:T(128)} %convert_element_type.168, () %tuple.39, bf16[192,2048]{1,0:T(8,128)(2,1)S(1)} %get-tuple-element.63), branch_computations={%region_8.8_spmd, %region_9.10_spmd} | conditional | flops 1594810368 | bytes 13320232 | solution.py:73
  303.8 1.1 compare_reduce_fusion.2
  305.5 6.3 %conditional.2 = (bf16[1,192,2048]{2,1,0:T(8,128)(2,1)S(1)}) conditional(s32[]{:T(128)} %convert_element_type.168, () %tuple.39, bf16[192,2048]{1,0:T(8,128)(2,1)S(1)} %get-tuple-element.63), branch_computations={%region_8.8_spmd, %region_9.10_spmd} | conditional | flops 1594810368 | bytes 13320232 | solution.py:73
  305.5 1.0 fusion.7
  313.5 2.7 copy.34
  316.2 3.7 all-to-all-start.1
  320.0 57.8 %all-to-all-done.1 = bf16[2,12,16,2048]{3,2,0,1:T(8,128)(2,1)S(1)} async-done(((bf16[2,12,16,2048]{3,2,0,1:T(8,128)(2,1)}), bf16[2,12,16,2048]{3,2,0,1:T(8,128)(2,1)S(1)}, u32[]{:S(2)}, u32[]{:S(2)}) %all-to-all-start.1) | async-done | bytes 1572896 | tf_op jit(solution)/shard_map/all_to_all | solution.py:104
  (68 shorter events, 19.4 us)
Async XLA Ops:
  7.2 62.7 %reduce-scatter.8.cloned.1.call-start = ((), (), s32[]{:S(2)}) async-start(), calls=%async_computation.5 | async-start | bytes 3538944 | tf_op jit(solution)/shard_map/reduce_scatter | solution.py:23
  7.9 94.7 %reduce-scatter.10.cloned.1.call-start = ((), (), s32[]{:S(2)}) async-start(), calls=%async_computation.7 | async-start | bytes 491520
  71.9 1.7 copy-start.3
  73.6 51.9 %copy-start.2 = (f32[24,16,32]{2,1,0:T(8,128)S(1)}, f32[24,16,32]{2,1,0:T(8,128)}, u32[]{:S(2)}) copy-start(f32[24,16,32]{2,1,0:T(8,128)} %param.8) | copy-start | bytes 147460
  73.6 50.7 %reduce-scatter.12.cloned.1.call-start = ((), (), s32[]{:S(2)}) async-start(), calls=%async_computation.8 | async-start | bytes 147456
  102.6 100.1 %all-gather.3.cloned.1.call-start = ((), (), s32[]{:S(2)}) async-start(), calls=%async_computation.6 | async-start | bytes 9437184 | tf_op jit(solution)/shard_map/all_gather | solution.py:36
  223.9 68.6 %all-to-all-start = ((bf16[2,12,16,2048]{3,2,0,1:T(8,128)(2,1)}), bf16[2,12,16,2048]{3,2,0,1:T(8,128)(2,1)}, u32[]{:S(2)}, u32[]{:S(2)}) async-start(bf16[2,12,16,2048]{3,2,0,1:T(8,128)(2,1)} %fusion.51), calls=%async_computation.1 | async-start | bytes 3145728 | tf_op jit(solution)/shard_map/all_to_all | solution.py:99
  294.1 1.7 copy-start
  302.1 1.7 copy-start.1
  303.8 1.7 copy-start
  311.8 1.7 copy-start.1
  316.2 61.6 %all-to-all-start.1 = ((bf16[2,12,16,2048]{3,2,0,1:T(8,128)(2,1)}), bf16[2,12,16,2048]{3,2,0,1:T(8,128)(2,1)S(1)}, u32[]{:S(2)}, u32[]{:S(2)}) async-start(bf16[2,12,16,2048]{3,2,0,1:T(8,128)(2,1)} %copy.34), calls=%async_computation.2 | async-start | bytes 3145728 | tf_op jit(solution)/shard_map/all_to_all | solution.py:104
Sparse Core Ops, SparseCore 0:
  11.1 58.7 reduce-scatter.7
  73.7 28.8 reduce-scatter.9
  105.6 18.6 reduce-scatter.11
  175.8 26.8 all-gather.2
where the time goes:
time: 387 us; the launch traced here: 386 us
  waiting for transfers between devices  256 us (66%)
  blocking collectives  49.5 us (13%)
  local copies, waits for them, and re-layouts  33.5 us (9%)
  starting transfers between devices  14.1 us (4%)
  between operations  13.9 us (4%)
  matrix products  9.09 us (2%)
  other arithmetic  7.46 us (2%)
    reduce_scatter x1, waiting for transfers between devices, sum_by_axis(): nearer = lax.psum_scatter(shard, axes[0], scatter_dimension=dim, tiled=True)  62 us
    all_to_all x1, waiting for transfers between devices, per_device(): lax.all_to_all(outgoing, 'dp', split_axis=1, concat_axis=1, tiled=True)  58.4 us
    all_to_all x1, waiting for transfers between devices, per_device(): lax.all_to_all(results, 'dp', split_axis=1, concat_axis=1, tiled=True)  57.8 us
    unnamed x6, waiting for transfers between devices  51 us
    all_gather x2, blocking collectives, all_blocks(): blocks = lax.all_gather(blocks, axes[k], axis=0, tiled=True)  49.5 us
    all_gather x1, waiting for transfers between devices, all_blocks(): blocks = lax.all_gather(blocks, axes[k], axis=0, tiled=True)  26.5 us
    all_to_all x1, starting transfers between devices, per_device(): lax.all_to_all(outgoing, 'dp', split_axis=1, concat_axis=1, tiled=True)  10.2 us
    reshape x1, local copies, waits for them, and re-layouts, laid_out(): blocks.reshape(*shape[:dim], shape[dim] * shape[dim + 1], *shape[dim + 2:])  8.54 us
  transfers between devices with their start and end apart: 6, of which 6 were waited for; matrix products, arithmetic and copies ran while one was open for 0% of the time, Pallas kernels for 0%

commit v1 on v0

v1 whole, which is shorter than its diff:
```python
import math

import jax
import jax.numpy as jnp
from jax import lax
from jax.experimental import pallas as pl
from jax.experimental.pallas import tpu as pltpu
from jax.sharding import Mesh
from jax.sharding import PartitionSpec as P

ITERS = 5
COLS = ("rep", "x1", "x0", "c")
CHIPS = ("rep", "x1", "x0")
OWNERS = ("rep", "x1")
SLOTS = 16
STEP = 4

decay_rate = 0.95
first_coef = 3.4445
second_coef = -4.775
third_coef = 2.0315
norm_eps = 1e-07

bf16 = jnp.bfloat16
f32 = jnp.float32
i32 = jnp.int32


def whole(space=pltpu.VMEM):
    return pl.BlockSpec(memory_space=space)


def pack_body(holder, *refs):
    grads, mom, out = refs[:STEP], refs[STEP], refs[STEP + 1]
    step = pl.program_id(0)
    rep, x1 = lax.axis_index("rep"), lax.axis_index("x1")
    x0, c = lax.axis_index("x0"), lax.axis_index("c")
    group = lax.broadcasted_iota(i32, (16, 128), 1) // 32
    spot = (rep % 2) * 2 + x1
    start = pl.multiple_of((rep // 2) * 128, 128)
    for k in range(STEP):
        for yy in range(4):
            tiles = [grads[k][0, 0, :, (yy * 4 + t) * 128 : (yy * 4 + t + 1) * 128] for t in range(4)]
            for q in range(4):
                dealt = None
                for t in range(4):
                    turn = ((t - q) * 32) % 128
                    moved = pltpu.roll(tiles[t], turn, 1) if turn else tiles[t]
                    dealt = moved if dealt is None else jnp.where(group == t, moved, dealt)
                out[q % 2, 2 * k + q // 2, :, yy * 128 : (yy + 1) * 128] = dealt.astype(bf16)
        own = mom[holder[step * STEP + k]] * decay_rate
        own = jnp.concatenate([own] * 4, axis=1)
        own = jnp.where(group == spot, own, 0.0)
        at = (c, 2 * k + x0, slice(None), pl.ds(start, 128))
        out[at] = (out[at].astype(f32) + own).astype(bf16)


def pack(grad_parts, momentum, holder):
    _, mats, rows, cols = grad_parts.shape
    picks = [
        pl.BlockSpec((1, 1, rows, cols), lambda i, h, k=k: (0, h[i * STEP + k], 0, 0)) for k in range(STEP)
    ]
    return pl.pallas_call(
        pack_body,
        grid_spec=pltpu.PrefetchScalarGridSpec(
            num_scalar_prefetch=1,
            grid=(SLOTS // STEP,),
            in_specs=picks + [pl.BlockSpec(momentum.shape, lambda i, h: (0, 0, 0))],
            out_specs=pl.BlockSpec((2, 2 * STEP, rows, cols // 4), lambda i, h: (0, i, 0, 0)),
        ),
        out_shape=jax.ShapeDtypeStruct((2, 2 * SLOTS, rows, cols // 4), bf16),
        name="pack",
    )(holder, *[grad_parts] * STEP, momentum)


def total_body(parts, out):
    total = jnp.sum(parts[...].astype(f32), axis=0).astype(bf16)
    for z in range(out.shape[0]):
        out[z] = total


def total(parts, copies):
    return pl.pallas_call(
        total_body,
        in_specs=[whole()],
        out_specs=whole(),
        out_shape=jax.ShapeDtypeStruct((copies,) + parts.shape[1:], bf16),
        name="total",
    )(parts)


def gram_body(source, out):
    s = source[...].reshape(out.shape[0], -1)
    out[...] = lax.dot_general(s, s, (((1,), (1,)), ((), ())), preferred_element_type=f32)


def gram(source):
    rows = source.shape[0] * source.shape[1]
    return pl.pallas_call(
        gram_body,
        in_specs=[whole()],
        out_specs=whole(),
        out_shape=jax.ShapeDtypeStruct((rows, rows), f32),
        name="gram",
    )(source)


def halves(a):
    high = a.astype(bf16)
    return high, (a - high.astype(f32)).astype(bf16)


def dot(a, b):
    return jnp.dot(a, b, preferred_element_type=f32)


def dot3(a, b):
    return dot(a[0], b[0]) + (dot(a[0], b[1]) + dot(a[1], b[0]))


def schulz_body(gram_a, gram_b, source, out):
    g = gram_a[...] + gram_b[...]
    rows = g.shape[0]
    own_rows = source.shape[1]
    z = lax.axis_index("dp")
    row = lax.broadcasted_iota(i32, g.shape, 0)
    col = lax.broadcasted_iota(i32, g.shape, 1)
    eye = row == col
    square = jnp.sum(jnp.sum(jnp.where(eye, g, 0.0), axis=1, keepdims=True), axis=0, keepdims=True)
    scale = 1.0 / (jnp.sqrt(square) + norm_eps)
    g = g * scale * scale
    pick = (
        lax.broadcasted_iota(i32, (own_rows, rows), 1)
        == lax.broadcasted_iota(i32, (own_rows, rows), 0) + z * own_rows
    )
    lead = pick.astype(bf16)
    lead = (lead, jnp.zeros_like(lead))
    for iteration in range(ITERS):
        gh = halves(g)
        w = second_coef * g + third_coef * dot3(gh, gh)
        w = w + jnp.where(eye, first_coef, 0.0)
        wh = halves(w)
        led = dot3(lead, wh)
        if iteration + 1 < ITERS:
            g = dot3(halves(dot3(wh, gh)), wh)
            lead = halves(led)
    lead = halves(led * (scale * math.sqrt(2048.0)))
    s = source[...].reshape(rows, -1)
    result = dot(lead[0], s) + dot(lead[1], s)
    own = source[z].astype(f32)
    lane = lax.broadcasted_iota(i32, (own_rows, 128), 1)
    for j in range(out.shape[0]):
        yy, t = j // 4, j % 4
        up = result[:, yy * 128 : (yy + 1) * 128]
        low = own[:, yy * 128 : (yy + 1) * 128]
        up = pltpu.roll(up, 128 - 32 * t, 1) if t else up
        low = pltpu.roll(low, (160 - 32 * t) % 128, 1) if t != 1 else low
        out[j] = jnp.where(lane < 32, up, low).astype(bf16)


def schulz(gram_a, gram_b, source):
    return pl.pallas_call(
        schulz_body,
        in_specs=[whole(), whole(), whole()],
        out_specs=whole(),
        out_shape=jax.ShapeDtypeStruct((SLOTS, source.shape[1], 128), bf16),
        name="schulz",
    )(gram_a, gram_b, source)


def place_body(slot, came, mom_in, orth_in, mom, orth):
    for m in range(mom.shape[0]):
        s = slot[m]
        here = (s >= 0) & (s < SLOTS)
        got = came[jnp.clip(s, 0, SLOTS - 1)].astype(f32)
        mom[m] = jnp.where(here, pltpu.roll(got, 96, 1)[:, :32], mom_in[m])
        orth[m] = jnp.where(here, got[:, :32], orth_in[m].astype(f32)).astype(bf16)


def place(slot, came, mom_in, orth_in):
    return pl.pallas_call(
        place_body,
        in_specs=[whole(pltpu.SMEM), whole(), whole(), whole()],
        out_specs=[whole(), whole()],
        out_shape=[jax.ShapeDtypeStruct(mom_in.shape, f32), jax.ShapeDtypeStruct(mom_in.shape, bf16)],
        name="place",
    )(slot, came, mom_in, orth_in)


def swapped(x, axis):
    return lax.ppermute(x, axis, [(0, 1), (1, 0)])


def one_pass(grad_parts, momentum, holder, slot, mom_in, orth_in):
    packed = pack(grad_parts, momentum, holder)
    both = lax.all_to_all(packed, "c", 0, 0, tiled=True)
    chip_sum = (both[0].astype(f32) + both[1].astype(f32)).astype(bf16)
    parts = lax.all_to_all(chip_sum, CHIPS, 0, 0, tiled=True)
    copies = total(parts, lax.axis_size("dp"))
    source = lax.all_to_all(copies, "dp", 0, 0, tiled=True)
    partial = gram(source)
    partial = partial + swapped(partial, "c")
    update = schulz(partial, swapped(partial, "x0"), source)
    came = lax.all_to_all(update, OWNERS, 0, 0, tiled=True)
    return place(slot, came, mom_in, orth_in)


def per_device(grad_parts, momentum, layer_live):
    mats = layer_live.shape[0]
    ids = jnp.arange(mats, dtype=i32)
    live = layer_live > 0
    rank = jnp.sum(jnp.where(live[None, :] & (ids[None, :] < ids[:, None]), 1, 0), axis=1)
    slot = jnp.where(live, rank, -1)
    places = jnp.arange(2 * SLOTS, dtype=i32)
    holder = jnp.sum(jnp.where(slot[None, :] == places[:, None], ids[None, :], 0), axis=1)
    orth = jnp.zeros(momentum.shape, bf16)
    mom, orth = one_pass(grad_parts, momentum, holder[:SLOTS], slot, momentum, orth)

    def again(mom, orth):
        return tuple(one_pass(grad_parts, momentum, holder[SLOTS:], slot - SLOTS, mom, orth))

    return lax.cond(jnp.sum(live.astype(i32)) > SLOTS, again, lambda mom, orth: (mom, orth), mom, orth)


def solution(mesh):
    torus = Mesh(
        mesh.devices.reshape(mesh.shape["dp"], mesh.shape["rep"], 2, 2, 2),
        ("dp", "rep", "x1", "x0", "c"),
    )
    return jax.shard_map(
        per_device,
        mesh=torus,
        in_specs=(P(COLS, None, "dp", None), P(None, "dp", COLS), P()),
        out_specs=(P(None, "dp", COLS), P(None, "dp", COLS)),
        check_vma=False,
    )
```

time: 387 us -> 110 us (0.28)
  waiting for transfers between devices: 256 us -> 17.4 us
  local copies, waits for them, and re-layouts: 33.5 us -> 0.67 us
  Pallas kernels: 0 us -> 16.2 us
  between operations: 13.9 us -> 1.25 us
  blocking collectives: 49.5 us -> 61.3 us
  matrix products: 9.09 us -> 0 us
  starting transfers between devices: 14.1 us -> 9.54 us
  other arithmetic: 7.46 us -> 3.29 us
    all_to_all x2 -> x1, waiting for transfers between devices: 116 us -> 9.98 us  [one_pass(): came = lax.all_to_all(update, OWNERS, 0, 0, tiled=True)]
    reduce_scatter x1 -> x0, waiting for transfers between devices: 62 us -> none  [sum_by_axis(): nearer = lax.psum_scatter(shard, axes[0], scatter_dimension=dim, tiled=True)]
    all_to_all x0 -> x3, blocking collectives: none -> 61.3 us  [the longest x1 30.6 us: one_pass(): parts = lax.all_to_all(chip_sum, CHIPS, 0, 0, tiled=True)]
    unnamed x6 -> x0, waiting for transfers between devices: 51 us -> none
    all_gather x2 -> x0, blocking collectives: 49.5 us -> none  [all_blocks(): blocks = lax.all_gather(blocks, axes[k], axis=0, tiled=True)]
    all_gather x1 -> x0, waiting for transfers between devices: 26.5 us -> none  [all_blocks(): blocks = lax.all_gather(blocks, axes[k], axis=0, tiled=True)]
    pallas_call x0 -> x5, Pallas kernels: none -> 16.2 us  [the longest x1 5.97 us: schulz(): pl.pallas_call(schulz_body, in_specs=[whole(), whole(), whole()], out_spe...]
    reshape x2 -> x0, local copies, waits for them, and re-layouts: 11.3 us -> none  [the longest x1 8.54 us: laid_out(): blocks.reshape(*shape[:dim], shape[dim] * shape[dim + 1], *shape[dim + 2:])]
  transfers between devices with their start and end apart: 6 -> 3, of which waited for: 6 -> 3; matrix products, arithmetic and copies ran while one was open for 0% -> 0% of each run, Pallas kernels for 0% -> 0%
where the time goes in v1:
time: 110 us
  blocking collectives  61.3 us (56%)
  waiting for transfers between devices  17.4 us (16%)
  Pallas kernels  16.2 us (15%)
  starting transfers between devices  9.54 us (9%)
  other arithmetic  3.29 us (3%)
  between operations  1.25 us (1%)
    all_to_all x1, blocking collectives, one_pass(): parts = lax.all_to_all(chip_sum, CHIPS, 0, 0, tiled=True)  30.6 us
    all_to_all x1, blocking collectives, one_pass(): source = lax.all_to_all(copies, 'dp', 0, 0, tiled=True)  25 us
    all_to_all x1, waiting for transfers between devices, one_pass(): came = lax.all_to_all(update, OWNERS, 0, 0, tiled=True)  9.98 us
    ppermute x2, waiting for transfers between devices, swapped(): return lax.ppermute(x, axis, [(0, 1), (1, 0)])  7.45 us
    pallas_call x1, Pallas kernels, schulz(): pl.pallas_call(schulz_body, in_specs=[whole(), whole(), whole()], out_spe...  5.97 us
    all_to_all x1, blocking collectives, one_pass(): both = lax.all_to_all(packed, 'c', 0, 0, tiled=True)  5.68 us
    ppermute x2, starting transfers between devices, swapped(): return lax.ppermute(x, axis, [(0, 1), (1, 0)])  5.01 us
    pallas_call x1, Pallas kernels, pack(): pl.pallas_call(pack_body, grid_spec=pltpu.PrefetchScalarGridSpec(num_scal...  4.87 us
  transfers between devices with their start and end apart: 3, of which 3 were waited for; matrix products, arithmetic and copies ran while one was open for 0% of the time, Pallas kernels for 0%

profile of v1, /device:TPU:2, one launch (start us, length us, event | category | flops | bytes accessed | tf_op | source)
XLA Modules:
  0.0 109.7 jit_solution(5604263943310563906)
XLA Ops:
  0.6 0.7 broadcast_compare_fusion
  1.3 0.1 select_reduce_fusion.1
  1.4 1.3 %broadcast_select_fusion = (s32[24]{0:T(128)S(1)}, s32[]{:T(128)}) fusion(s32[24]{0:T(128)S(1)} %select_reduce_fusion.1, s32[24]{0:T(128)} %param.7), kind=kLoop, calls=%fused_computation.11 | loop fusion | flops 95 | bytes 292 | tf_op jit(solution)/shard_map/jit(_where)/select_n | solution.py:213
  2.7 0.1 select_reduce_fusion
  2.8 4.9 %pack.3 = bf16[2,32,16,512]{3,2,1,0:T(8,128)(2,1)} custom-call(s32[16]{0:T(128)S(1)} %bitcast.5, f32[1,24,16,2048]{3,2,1,0:T(8,128)} %refs_3_.1, f32[1,24,16,2048]{3,2,1,0:T(8,128)} %refs_3_.1, f32[1,24,16,2048]{3,2,1,0:T(8,128)} %refs_3_.1, f32[1,24,16,2048]{3,2,1,0:T(8,128)} %refs_3_.1, f32[24,16,32]{2,1,0:T(8,128)} %mom_in.1), custom_call_target="tpu_custom_call" | custom-call | tf_op jit(solution)/shard_map/pack/pallas_call | solution.py:63
  7.7 5.7 %all_to_all.39 = bf16[2,32,16,512]{3,2,1,0:T(8,128)(2,1)S(1)} all-to-all(bf16[2,32,16,512]{3,2,1,0:T(8,128)(2,1)} %pack.3), channel_id=1, replica_groups=mesh['dp'=12,'rep'=8,'x1'=2,'x0'=2,'c'=2] {'c'}, dimensions={0} | all-to-all | bytes 2097152 | tf_op jit(solution)/shard_map/all_to_all | solution.py:196
  13.3 0.2 fusion.1
  13.5 30.6 %all_to_all.40.parts = bf16[32,16,512]{2,1,0:T(8,128)(2,1)} all-to-all(bf16[32,16,512]{2,1,0:T(8,128)(2,1)S(1)} %fusion.1), channel_id=1, replica_groups=mesh['dp'=12,'rep'=8,'x1'=2,'x0'=2,'c'=2] {'rep','x1','x0'}, dimensions={0} | all-to-all | bytes 1048576 | tf_op jit(solution)/shard_map/all_to_all | solution.py:198
  44.1 1.8 %total.3 = bf16[12,16,512]{2,1,0:T(8,128)(2,1)} custom-call(bf16[32,16,512]{2,1,0:T(8,128)(2,1)} %all_to_all.40.parts), custom_call_target="tpu_custom_call" | custom-call | tf_op jit(solution)/shard_map/total/pallas_call | solution.py:83
  45.9 25.0 %all_to_all.41.source = bf16[12,16,512]{2,1,0:T(8,128)(2,1)} all-to-all(bf16[12,16,512]{2,1,0:T(8,128)(2,1)} %total.3), channel_id=1, replica_groups=mesh['dp'=12,'rep'=8,'x1'=2,'x0'=2,'c'=2] {'dp'}, dimensions={0} | all-to-all | bytes 393216 | tf_op jit(solution)/shard_map/all_to_all | solution.py:200
  71.0 1.8 %gram.3 = f32[192,192]{1,0:T(8,128)} custom-call(bf16[12,16,512]{2,1,0:T(8,128)(2,1)} %all_to_all.41.source), custom_call_target="tpu_custom_call" | custom-call | tf_op jit(solution)/shard_map/gram/pallas_call | solution.py:99
  72.8 1.9 %collective-permute-start.2 = (f32[192,192]{1,0:T(8,128)}, f32[192,192]{1,0:T(8,128)S(1)}, u32[]{:S(2)}, u32[]{:S(2)}) collective-permute-start(f32[192,192]{1,0:T(8,128)} %gram.3), channel_id=1, source_target_pairs={{0,1},{1,0},{2,3},{3,2},{4,5},{5,4},{6,7},{7,6},{8,9},{9,8},{10,11... | collective-permute-start | bytes 442376 | tf_op jit(solution)/shard_map/ppermute | solution.py:191
  74.7 1.6 %collective-permute-done.2 = f32[192,192]{1,0:T(8,128)S(1)} collective-permute-done((f32[192,192]{1,0:T(8,128)}, f32[192,192]{1,0:T(8,128)S(1)}, u32[]{:S(2)}, u32[]{:S(2)}) %collective-permute-start.2) | collective-permute-done | bytes 147488 | tf_op jit(solution)/shard_map/ppermute | solution.py:191
  76.3 1.0 add.16.gram_a
  77.3 0.0 copy-start.3
  77.3 3.1 %collective-permute-start.3 = (f32[192,192]{1,0:T(8,128)S(1)}, f32[192,192]{1,0:T(8,128)}, u32[]{:S(2)}, u32[]{:S(2)}) collective-permute-start(f32[192,192]{1,0:T(8,128)S(1)} %add.16.gram_a), channel_id=1, source_target_pairs={{0,2},{2,0},{1,3},{3,1},{4,6},{6,4},{5,7},{7,5},{8,10},{10,8},{9,1... | collective-permute-start | bytes 442376 | tf_op jit(solution)/shard_map/ppermute | solution.py:191
  80.4 5.8 %collective-permute-done.3.gram_b = f32[192,192]{1,0:T(8,128)} collective-permute-done((f32[192,192]{1,0:T(8,128)S(1)}, f32[192,192]{1,0:T(8,128)}, u32[]{:S(2)}, u32[]{:S(2)}) %collective-permute-start.3) | collective-permute-done | bytes 147488 | tf_op jit(solution)/shard_map/ppermute | solution.py:191
  86.2 0.0 copy-done.3
  86.2 6.0 %schulz.3 = bf16[16,16,128]{2,1,0:T(8,128)(2,1)} custom-call(f32[192,192]{1,0:T(8,128)} %copy-done.3, f32[192,192]{1,0:T(8,128)} %collective-permute-done.3.gram_b, bf16[12,16,512]{2,1,0:T(8,128)(2,1)} %all_to_all.41.source), custom_call_target="tpu_custom_call" | custom-call | tf_op jit(solution)/shard_map/schulz/pallas_call | solution.py:162
  92.2 4.5 %all-to-all-start.7 = ((bf16[16,16,128]{2,1,0:T(8,128)(2,1)}), bf16[16,16,128]{2,1,0:T(8,128)(2,1)S(1)}, u32[]{:S(2)}, u32[]{:S(2)}) async-start(bf16[16,16,128]{2,1,0:T(8,128)(2,1)} %schulz.3), calls=%async_computation.7 | async-start | bytes 131072 | tf_op jit(solution)/shard_map/all_to_all | solution.py:204
  97.3 10.0 %all-to-all-done.7.came = bf16[16,16,128]{2,1,0:T(8,128)(2,1)S(1)} async-done(((bf16[16,16,128]{2,1,0:T(8,128)(2,1)}), bf16[16,16,128]{2,1,0:T(8,128)(2,1)S(1)}, u32[]{:S(2)}, u32[]{:S(2)}) %all-to-all-start.7) | async-done | bytes 65568 | tf_op jit(solution)/shard_map/all_to_all | solution.py:204
  107.3 0.7 broadcast_in_dim.38.orth_in
  108.0 0.0 copy-done.4
  108.0 1.7 %place.3 = (f32[24,16,32]{2,1,0:T(8,128)}, bf16[24,16,32]{2,1,0:T(8,128)(2,1)}) custom-call(s32[24]{0:T(128)S(1)} %get-tuple-element.34.slot, bf16[16,16,128]{2,1,0:T(8,128)(2,1)} %copy-done.4, f32[24,16,32]{2,1,0:T(8,128)S(1)} %copy-done.1, bf16[24,16,32]{2,1,0:T(8,128)(2,1)} %broadcast_in_dim.38.orth_in), custom_call_target="tpu_custom_call" | custom-call | tf_op jit(solution)/shard_map/place/pallas_call | solution.py:181
  (6 shorter events, 0.0 us)
Async XLA Ops:
  13.3 94.6 %copy-start.1 = (f32[24,16,32]{2,1,0:T(8,128)S(1)}, f32[24,16,32]{2,1,0:T(8,128)}, u32[]{:S(2)}) copy-start(f32[24,16,32]{2,1,0:T(8,128)} %mom_in.1) | copy-start | bytes 147460
  13.3 96.4 %copy-start = (f32[1,24,16,2048]{3,2,1,0:T(8,128)S(1)}, f32[1,24,16,2048]{3,2,1,0:T(8,128)}, u32[]{:S(2)}) copy-start(f32[1,24,16,2048]{3,2,1,0:T(8,128)} %refs_3_.1) | copy-start | bytes 9437188
  72.8 3.5 %collective-permute-start.2 = (f32[192,192]{1,0:T(8,128)}, f32[192,192]{1,0:T(8,128)S(1)}, u32[]{:S(2)}, u32[]{:S(2)}) collective-permute-start(f32[192,192]{1,0:T(8,128)} %gram.3), channel_id=1, source_target_pairs={{0,1},{1,0},{2,3},{3,2},{4,5},{5,4},{6,7},{7,6},{8,9},{9,8},{10,11... | collective-permute-start | bytes 442376 | tf_op jit(solution)/shard_map/ppermute | solution.py:191
  77.3 9.0 %copy-start.3 = (f32[192,192]{1,0:T(8,128)}, f32[192,192]{1,0:T(8,128)S(1)}, u32[]{:S(2)}) copy-start(f32[192,192]{1,0:T(8,128)S(1)} %add.16.gram_a) | copy-start | bytes 442372
  77.3 8.9 %collective-permute-start.3 = (f32[192,192]{1,0:T(8,128)S(1)}, f32[192,192]{1,0:T(8,128)}, u32[]{:S(2)}, u32[]{:S(2)}) collective-permute-start(f32[192,192]{1,0:T(8,128)S(1)} %add.16.gram_a), channel_id=1, source_target_pairs={{0,2},{2,0},{1,3},{3,1},{4,6},{6,4},{5,7},{7,5},{8,10},{10,8},{9,1... | collective-permute-start | bytes 442376 | tf_op jit(solution)/shard_map/ppermute | solution.py:191
  92.2 15.1 %all-to-all-start.7 = ((bf16[16,16,128]{2,1,0:T(8,128)(2,1)}), bf16[16,16,128]{2,1,0:T(8,128)(2,1)S(1)}, u32[]{:S(2)}, u32[]{:S(2)}) async-start(bf16[16,16,128]{2,1,0:T(8,128)(2,1)} %schulz.3), calls=%async_computation.7 | async-start | bytes 131072 | tf_op jit(solution)/shard_map/all_to_all | solution.py:204
  107.3 0.7 copy-start.4
